TPU v7x, 32 devices: a whole 2x2x4 slice. The times are simulated.
32 devices in a mesh: ep: 8 (over z, y), fsdp: 4 (over x, core).
Axes of the slice: x: 2, y: 2, z: 4, core: 2. Of those that a mesh axis runs over, the one named last changes fastest.
Arguments:
- train_gate: float32 [64, 2048, 1024], P('ep', 'fsdp'), may hold values from -0.1875 to 0.1875
- other_gate: float32 [64, 2048, 1024], P('ep', 'fsdp'), may hold values from -0.125 to 0.125
- train_up: float32 [64, 2048, 1024], P('ep', 'fsdp'), may hold values from -0.1875 to 0.1875
- other_up: float32 [64, 2048, 1024], P('ep', 'fsdp'), may hold values from -0.125 to 0.125
- mix_share: float32 [64], P('ep'), may hold values from 0.2 to 0.8
- router_weight: float32 [2048, 64], P('fsdp', 'ep'), may hold values from -0.125 to 0.125
- router_gain: float32 [2048], P('fsdp'), may hold values from 0.25 to 1.75
Outputs:
- ready_gate: bfloat16 [64, 2048, 1024], P('ep')
- ready_up: bfloat16 [64, 2048, 1024], P('ep')
- scale_gate: float32 [64, 1024], P('ep')
- scale_up: float32 [64, 1024], P('ep')
- serve_router: bfloat16 [2048, 64], replicated
All inputs are finite; a program needn't handle non-finite values. Where the computation divides by a largest or mean magnitude, that divisor is 1e-20 or more.
Results may differ from a plain program's by a relative error of at most 0.001.
Values may be sent and summed in bfloat16 or wider, within the bound.
A program may use at most 256 MiB of HBM per device.

v0:
```python
import jax
import jax.numpy as jnp
from jax import lax
from jax.sharding import PartitionSpec as P


def per_device(train_gate, other_gate, train_up, other_up, mix_share, router_weight, router_gain):
    latest_gate = (
        mix_share[:, None, None] * train_gate + (1.0 - mix_share[:, None, None]) * other_gate
    )
    latest_up = mix_share[:, None, None] * train_up + (1.0 - mix_share[:, None, None]) * other_up
    scale_gate, scale_up = lax.pmax(
        (jnp.max(jnp.abs(latest_gate), axis=1), jnp.max(jnp.abs(latest_up), axis=1)), "fsdp"
    )
    narrow_gate, narrow_up = (
        (latest_gate / jnp.expand_dims(scale_gate, 1)).astype(jnp.bfloat16),
        (latest_up / jnp.expand_dims(scale_up, 1)).astype(jnp.bfloat16),
    )
    ready_gate, ready_up = (
        lax.all_gather(narrow_gate, "fsdp", axis=1, tiled=True),
        lax.all_gather(narrow_up, "fsdp", axis=1, tiled=True),
    )
    part_router = (router_weight * router_gain[:, None]).astype(jnp.bfloat16)
    row_router = lax.all_gather(part_router, "fsdp", axis=0, tiled=True)
    serve_router = lax.all_gather(row_router, "ep", axis=1, tiled=True)
    return (ready_gate, ready_up, scale_gate, scale_up, serve_router)


def solution(mesh):
    placed = (
        P("ep", "fsdp", None),
        P("ep", "fsdp", None),
        P("ep", "fsdp", None),
        P("ep", "fsdp", None),
        P("ep"),
        P("fsdp", "ep"),
        P("fsdp"),
    )
    return jax.shard_map(
        per_device,
        mesh=mesh,
        in_specs=placed,
        out_specs=(P("ep", None, None), P("ep", None, None), P("ep", None), P("ep", None), P()),
        check_vma=False,
    )
```

profile of v0, /device:TPU:0, one launch (start us, length us, event | category | flops | bytes accessed | tf_op | source)
XLA Modules:
  0.0 555.3 jit_solution(14787650851884378681)
XLA Ops:
  7.2 0.0 all-reduce.3.cloned.1.call-start
  7.2 0.7 broadcast_subtract_fusion
  7.9 0.0 copy-start.3
  7.9 23.2 %abs_reduce_fusion = (f32[8,1024]{1,0:T(8,128)}, f32[8,1024]{1,0:T(8,128)}) fusion(f32[8,512,1024]{2,1,0:T(8,128)} %param.10, f32[8]{0:T(128)S(1)} %broadcast_subtract_fusion, f32[8,512,1024]{2,1,0:T(8,128)} %param.9, f32[8]{0:T(128)} %param.11, f32[8,512,1024]{2,1,0:T(8,128)} %param.8, f32[8,512,1024]{2,1,0:T(8,128)} %param.7), kind=kLoop, calls=%fused_computation.1 | loop fusion | flops 41926656 | bytes 67174464 | tf_op jit(solution)/shard_map/reduce_max | solution.py:13
  31.1 0.0 all-reduce.3.cloned.1.call-update
  31.1 0.0 all-gather.3.cloned.1.call-start
  31.2 34.4 %all-reduce.3.cloned.1.call-done = (f32[8,1024]{1,0:T(8,128)}, f32[8,1024]{1,0:T(8,128)}) async-done(((f32[8,1024]{1,0:T(8,128)}, f32[8,1024]{1,0:T(8,128)}), (f32[8,1024]{1,0:T(8,128)}, f32[8,1024]{1,0:T(8,128)})) %all-reduce.3.cloned.1.call-update) | async-done | bytes 65552 | tf_op jit(solution)/shard_map/pmax | solution.py:12
  65.6 0.0 copy-done.3
  65.6 29.4 %divide_convert_fusion = (bf16[8,512,1024]{2,1,0:T(8,128)(2,1)}, bf16[8,512,1024]{2,1,0:T(8,128)(2,1)}) fusion(f32[8,1024]{1,0:T(8,128)} %get-tuple-element.19, f32[8,512,1024]{2,1,0:T(8,128)} %param.10, f32[8]{0:T(128)S(1)} %broadcast_subtract_fusion, f32[8,512,1024]{2,1,0:T(8,128)} %param.9, f32[8]{0:T(128)S(1)} %copy-done.3, ...), kind=kLoop, calls=%fused_computation | loop fusion | flops 41943040 | bytes 83951680 | tf_op jit(solution)/shard_map/convert_element_type | solution.py:17
  95.0 0.0 copy-start.2
  95.0 0.0 copy-start.4
  95.0 0.0 all-gather.3.cloned.1.call-update
  95.0 0.0 all-gather.5.cloned.1.call-start
  95.0 0.7 all-gather.5.cloned.1.call-update
  95.7 0.0 copy-done.2
  95.7 0.0 copy-done.4
  95.8 5.2 all_gather.14
  101.0 30.9 %all_gather.15 = bf16[2048,64]{0,1:T(8,128)(2,1)S(1)} all-gather(bf16[2048,8]{0,1:T(8,128)(2,1)S(1)} %all_gather.14), channel_id=1, replica_groups=mesh['ep'=8,'fsdp'=4] {'ep'}, dimensions={1}, use_global_device_ids=true | all-gather | bytes 294912 | tf_op jit(solution)/shard_map/all_gather | solution.py:25
  131.8 164.8 %all-gather.3.cloned.1.call-done = bf16[8,2048,1024]{2,1,0:T(8,128)(2,1)} async-done(((bf16[8,512,1024]{2,1,0:T(8,128)(2,1)}), bf16[8,2048,1024]{2,1,0:T(8,128)(2,1)}) %all-gather.3.cloned.1.call-update) | async-done | bytes 33554448 | tf_op jit(solution)/shard_map/all_gather | solution.py:20
  296.7 203.7 %all-gather.5.cloned.1.call-done = bf16[8,2048,1024]{2,1,0:T(8,128)(2,1)} async-done(((bf16[8,512,1024]{2,1,0:T(8,128)(2,1)}), bf16[8,2048,1024]{2,1,0:T(8,128)(2,1)}) %all-gather.5.cloned.1.call-update) | async-done | bytes 33554448 | tf_op jit(solution)/shard_map/all_gather | solution.py:21
  500.4 23.2 %copy.17 = bf16[8,2048,1024]{2,1,0:T(8,128)(2,1)} copy(bf16[8,2048,1024]{2,1,0:T(8,128)(2,1)} %all-gather.3.cloned.1.call-done) | data formatting | bytes 67108864
  523.6 0.0 copy-start.1
  523.6 0.0 copy-start
  523.6 23.2 %copy.18 = bf16[8,2048,1024]{2,1,0:T(8,128)(2,1)} copy(bf16[8,2048,1024]{2,1,0:T(8,128)(2,1)} %all-gather.5.cloned.1.call-done) | data formatting | bytes 67108864
  546.8 0.0 copy-done.1
  546.8 0.6 copy.19
  547.4 0.0 copy-done
  547.5 0.6 copy.20
  548.1 0.7 copy.21
  (1 shorter events, 0.0 us)
Async XLA Ops:
  7.2 58.4 %all-reduce.3.cloned.1.call-start = ((), (), s32[]{:S(2)}) async-start(), calls=%async_computation.2 | async-start | bytes 131072 | tf_op jit(solution)/shard_map/pmax | solution.py:12
  7.9 57.7 %copy-start.3 = (f32[8]{0:T(128)S(1)}, f32[8]{0:T(128)}, u32[]{:S(2)}) copy-start(f32[8]{0:T(128)} %param.11) | copy-start | bytes 100
  31.1 265.5 %all-gather.3.cloned.1.call-start = ((), (), s32[]{:S(2)}) async-start(), calls=%async_computation | async-start | bytes 41943040 | tf_op jit(solution)/shard_map/all_gather | solution.py:20
  95.0 0.8 copy-start.2
  95.0 0.8 copy-start.4
  95.0 405.4 %all-gather.5.cloned.1.call-start = ((), (), s32[]{:S(2)}) async-start(), calls=%async_computation.1 | async-start | bytes 41943040 | tf_op jit(solution)/shard_map/all_gather | solution.py:21
  523.6 23.3 %copy-start.1 = (f32[8,1024]{1,0:T(8,128)S(1)}, f32[8,1024]{1,0:T(8,128)}, u32[]{:S(2)}) copy-start(f32[8,1024]{1,0:T(8,128)} %get-tuple-element.18) | copy-start | bytes 98308
  523.6 23.9 %copy-start = (f32[8,1024]{1,0:T(8,128)S(1)}, f32[8,1024]{1,0:T(8,128)}, u32[]{:S(2)}) copy-start(f32[8,1024]{1,0:T(8,128)} %get-tuple-element.19) | copy-start | bytes 98308
Sparse Core Ops, SparseCore 0:
  31.2 34.2 all-reduce.2
  95.1 201.4 all-gather.2
  298.8 201.4 all-gather.4
where the time goes:
time: 556 us; the launch traced here: 555 us
  waiting for transfers between devices  404 us (73%)
  other arithmetic  53.3 us (10%)
  local copies, waits for them, and re-layouts  48.4 us (9%)
  blocking collectives  36.1 us (6%)
  between operations  13.8 us (2%)
    all_gather x1, waiting for transfers between devices, per_device(): lax.all_gather(narrow_up, 'fsdp', axis=1, tiled=True)  204 us
    all_gather x1, waiting for transfers between devices, per_device(): lax.all_gather(narrow_gate, 'fsdp', axis=1, tiled=True)  165 us
    unnamed x15, local copies, waits for them, and re-layouts  48.4 us
    pmax x1, waiting for transfers between devices, per_device(): lax.pmax((jnp.max(jnp.abs(latest_gate), axis=1), jnp.max(jnp.abs(latest_u...  34.4 us
    all_gather x1, blocking collectives, per_device(): serve_router = lax.all_gather(row_router, 'ep', axis=1, tiled=True)  30.9 us
    convert_element_type x1, other arithmetic, per_device(): (latest_up / jnp.expand_dims(scale_up, 1)).astype(jnp.bfloat16)  29.4 us
    reduce_max x1, other arithmetic, per_device(): jnp.max(jnp.abs(latest_up), axis=1)  23.2 us
  transfers between devices with their start and end apart: 3, of which 3 were waited for; matrix products, arithmetic and copies ran while one was open for 0% of the time, Pallas kernels for 0%

commit v1 on v0

v1 whole, which is shorter than its diff:
```python
import jax
import jax.numpy as jnp
from jax import lax
from jax.experimental import pallas as pl
from jax.sharding import PartitionSpec as P


def swap(value, axis, size, bit):
    return lax.ppermute(value, axis, [(i, i ^ bit) for i in range(size)])


def blank(shape):
    return pl.pallas_call(
        lambda out: None,
        out_shape=jax.ShapeDtypeStruct(shape, jnp.bfloat16),
        out_specs=pl.BlockSpec(memory_space=pl.ANY),
    )()


def bits_of(size):
    assert size & (size - 1) == 0
    return [1 << b for b in range(size.bit_length() - 1)]


def solution(mesh):
    fsdp, ep = mesh.shape["fsdp"], mesh.shape["ep"]
    rows_bits, ep_bits = bits_of(fsdp), bits_of(ep)

    def largest(value):
        others = [swap(value, "fsdp", fsdp, d) for d in range(1, fsdp)]
        for other in others:
            value = jnp.maximum(value, other)
        return value

    def double(value, axis, size, bit, done):
        other = swap(value, axis, size, bit)
        upper = (lax.axis_index(axis) & bit) != 0
        return jnp.stack([jnp.where(upper, other, value), jnp.where(upper, value, other)], axis=done)

    def per_device(train_gate, other_gate, train_up, other_up, mix_share, router_weight, router_gain):
        experts, depth, width = train_gate.shape
        me = lax.axis_index("fsdp")
        pairs = ((train_gate, other_gate), (train_up, other_up))
        chunks = [(e, w) for e in range(experts) for w in range(2)]

        def mixed(chunk, share):
            e, w = chunk
            train, other = pairs[w]
            return share[e] * train[e] + (1.0 - share[e]) * other[e]

        def tops(group, share):
            return jnp.stack([jnp.max(jnp.abs(mixed(c, share)), axis=0) for c in group])

        def narrow(chunk, share, scale):
            return (mixed(chunk, share) / scale[None]).astype(jnp.bfloat16)

        total = len(chunks)
        cuts = [min(c, total) for c in (0, 2, 7)] + [total]
        groups = [chunks[i:j] for i, j in zip(cuts, cuts[1:]) if j > i]
        share, scales, owns, crossed = mix_share, [], [], []
        top_bit, low_bits = rows_bits[-1], rows_bits[:-1][::-1]

        def send(n):
            crossed.append(swap(owns[n], "fsdp", fsdp, top_bit))

        local = tops(groups[0], share)
        share, local = lax.optimization_barrier((share, local))
        scale = largest(local)
        for g, group in enumerate(groups):
            scales.append(scale)
            for i, c in enumerate(group):
                n = len(owns)
                if n >= 4:
                    share, crossed[n - 4] = lax.optimization_barrier((share, crossed[n - 4]))
                own = narrow(c, share, scale[i])
                share, own = lax.optimization_barrier((share, own))
                if n >= 2:
                    crossed[n - 2], own = lax.optimization_barrier((crossed[n - 2], own))
                owns.append(own)
                send(n)
                if i == 0 and g + 1 < len(groups):
                    local = tops(groups[g + 1], share)
                    share, local = lax.optimization_barrier((share, local))
                    ahead = largest(local)
            if g + 1 < len(groups):
                scale = ahead

        def across(held):
            for bit in low_bits:
                held = held + [(place ^ bit, swap(piece, "fsdp", fsdp, bit)) for place, piece in held]
            return held

        def put(out, e, held):
            for place, piece in held:
                out = lax.dynamic_update_slice(out, piece[None, None], (e, place, 0, 0))
            return out

        outs = [blank((experts, fsdp, depth, width)) for _ in range(2)]
        for n in range(total):
            e, w = chunks[n]
            outs[w] = put(outs[w], e, across([(me, owns[n])]))
            outs[w] = put(outs[w], e, across([(me ^ top_bit, crossed[n])]))
        ready = [o.reshape(experts, fsdp * depth, width) for o in outs]
        scales = jnp.concatenate(scales, axis=0).reshape(experts, 2, width)

        whole = (router_weight * router_gain[:, None]).astype(jnp.bfloat16).T
        wide = whole.shape
        for done, bit in enumerate(rows_bits[::-1]):
            whole = double(whole, "fsdp", fsdp, bit, done)
            if done == 0:
                whole, _ = lax.optimization_barrier((whole, crossed[total // 2]))
        whole = jnp.moveaxis(whole.reshape(fsdp, *wide), 0, 1).reshape(wide[0], fsdp * wide[1])
        for done, bit in enumerate(ep_bits[::-1]):
            whole = double(whole, "ep", ep, bit, done)
        whole = whole.reshape(ep * wide[0], fsdp * wide[1])
        return ready[0], ready[1], scales[:, 0], scales[:, 1], whole.T

    placed = (
        P("ep", "fsdp", None),
        P("ep", "fsdp", None),
        P("ep", "fsdp", None),
        P("ep", "fsdp", None),
        P("ep"),
        P("fsdp", "ep"),
        P("fsdp"),
    )
    return jax.shard_map(
        per_device,
        mesh=mesh,
        in_specs=placed,
        out_specs=(P("ep", None, None), P("ep", None, None), P("ep", None), P("ep", None), P()),
        check_vma=False,
    )
```

time: 556 us -> 461 us (0.83)
  waiting for transfers between devices: 404 us -> 181 us
  local copies, waits for them, and re-layouts: 48.4 us -> 125 us
  other arithmetic: 53.3 us -> 101 us
  blocking collectives: 36.1 us -> 0 us
  starting transfers between devices: 0.12 us -> 35.4 us
    all_gather x2 -> x0, waiting for transfers between devices: 369 us -> none  [the longest x1 204 us: per_device(): lax.all_gather(narrow_up, 'fsdp', axis=1, tiled=True)]
    ppermute x0 -> x62, waiting for transfers between devices: none -> 181 us  [swap(): return lax.ppermute(value, axis, [(i, i ^ bit) for i in range(size)])]
    dynamic_update_slice x0 -> x64, local copies, waits for them, and re-layouts: none -> 113 us  [put(): out = lax.dynamic_update_slice(out, piece[None, None], (e, place, 0, 0))]
    unnamed x15 -> x14, local copies, waits for them, and re-layouts: 48.4 us -> 1.92 us
    all_gather x2 -> x0, blocking collectives: 36.1 us -> none  [the longest x1 30.9 us: per_device(): serve_router = lax.all_gather(row_router, 'ep', axis=1, tiled=True)]
    ppermute x0 -> x62, starting transfers between devices: none -> 35.4 us  [swap(): return lax.ppermute(value, axis, [(i, i ^ bit) for i in range(size)])]
    pmax x1 -> x0, waiting for transfers between devices: 34.4 us -> none  [per_device(): lax.pmax((jnp.max(jnp.abs(latest_gate), axis=1), jnp.max(jnp.abs(latest_u...]
    convert_element_type x2 -> x16, other arithmetic: 29.4 us -> 60 us  [narrow(): return (mixed(chunk, share) / scale[None]).astype(jnp.bfloat16)]
  transfers between devices with their start and end apart: 3 -> 62, of which waited for: 3 -> 18; matrix products, arithmetic and copies ran while one was open for 0% -> 48% of each run, Pallas kernels for 0% -> 0%
where the time goes in v1:
time: 461 us; the launch traced here: 459 us
  waiting for transfers between devices  181 us (39%)
  local copies, waits for them, and re-layouts  125 us (27%)
  other arithmetic  101 us (22%)
  starting transfers between devices  35.4 us (8%)
  between operations  16.1 us (3%)
    ppermute x62, waiting for transfers between devices, swap(): return lax.ppermute(value, axis, [(i, i ^ bit) for i in range(size)])  181 us
    dynamic_update_slice x64, local copies, waits for them, and re-layouts, put(): out = lax.dynamic_update_slice(out, piece[None, None], (e, place, 0, 0))  113 us
    convert_element_type x16, other arithmetic, narrow(): return (mixed(chunk, share) / scale[None]).astype(jnp.bfloat16)  60 us
    reduce_max x6, other arithmetic, tops(): return jnp.stack([jnp.max(jnp.abs(mixed(c, share)), axis=0) for c in group])  39.9 us
    ppermute x62, starting transfers between devices, swap(): return lax.ppermute(value, axis, [(i, i ^ bit) for i in range(size)])  35.4 us
    slice x16, local copies, waits for them, and re-layouts, mixed(): return share[e] * train[e] + (1.0 - share[e]) * other[e]  9.53 us
  transfers between devices with their start and end apart: 62, of which 18 were waited for; matrix products, arithmetic and copies ran while one was open for 48% of the time, Pallas kernels for 0%

profile of v1, /device:TPU:0, one launch (start us, length us, event | category | flops | bytes accessed | tf_op | source)
XLA Modules:
  0.0 458.6 jit_solution(18049959172221683288)
XLA Ops:
  1.3 4.7 %abs_reduce_fusion.14 = (f32[1024]{0:T(1024)S(1)}, f32[1024]{0:T(1024)S(1)}) fusion(f32[8,512,1024]{2,1,0:T(8,128)} %param.10, f32[8,512,1024]{2,1,0:T(8,128)} %param.9, f32[]{:T(128)S(6)} %sub.82, f32[]{:T(128)} %bitcast.304, f32[8,512,1024]{2,1,0:T(8,128)} %param.8, f32[8,512,1024]{2,1,0:T(8,128)} %param.7), kind=kLoop, calls=%fused_computation.46 | loop fusion | flops 5240832 | bytes 8396808 | tf_op jit(solution)/shard_map/reduce_max | solution.py:52
  17.5 5.3 %abs_reduce_fusion.10 = (f32[1024]{0:T(1024)S(1)}, f32[1024]{0:T(1024)S(1)}) fusion(f32[8,512,1024]{2,1,0:T(8,128)} %param.10, f32[8,512,1024]{2,1,0:T(8,128)} %param.9, f32[]{:T(128)S(6)} %sub.85, f32[]{:T(128)} %bitcast.11, f32[]{:T(128)S(6)} %sub.84, f32[]{:T(128)} %bitcast.8), kind=kLoop, calls=%fused_computation.42 | loop fusion | flops 5240832 | bytes 8396816 | tf_op jit(solution)/shard_map/reduce_max | solution.py:52
  22.8 7.7 %abs_reduce_fusion.9 = (f32[1024]{0:T(1024)S(1)}, f32[1024]{0:T(1024)S(1)}, f32[1024]{0:T(1024)S(1)}) fusion(f32[8,512,1024]{2,1,0:T(8,128)} %param.8, f32[8,512,1024]{2,1,0:T(8,128)} %param.7, f32[]{:T(128)S(6)} %sub.86, f32[]{:T(128)} %bitcast.14, f32[]{:T(128)S(6)} %sub.85, f32[]{:T(128)} %bitcast.11, f32[]{:T(128)S(6)} %sub.84, f32[]{:T(128)} %bitcast.8), kind=kLoop, calls=%fused_computation.41 | loop fusion | flops 7861248 | bytes 12595224 | tf_op jit(solution)/shard_map/reduce_max | solution.py:52
  39.4 3.4 fusion.13
  49.9 9.5 %abs_reduce_fusion.1 = (f32[1024]{0:T(1024)S(1)}, f32[1024]{0:T(1024)S(1)}, f32[1024]{0:T(1024)S(1)}, f32[1024]{0:T(1024)S(1)}) fusion(f32[8,512,1024]{2,1,0:T(8,128)} %param.8, f32[8,512,1024]{2,1,0:T(8,128)} %param.7, f32[]{:T(128)S(6)} %sub.93, f32[]{:T(128)} %bitcast.33, f32[]{:T(128)S(6)} %sub.91, f32[]{:T(128)} %bitcast.27, f32[]{:T(128)S(6)} %sub.90, ...), kind=kLoop, calls=%fused_computation.33 | loop fusion | flops 10481664 | bytes 16793632 | tf_op jit(solution)/shard_map/reduce_max | solution.py:52
  59.4 9.6 %abs_reduce_fusion = (f32[1024]{0:T(1024)S(1)}, f32[1024]{0:T(1024)S(1)}, f32[1024]{0:T(1024)S(1)}, f32[1024]{0:T(1024)S(1)}) fusion(f32[8,512,1024]{2,1,0:T(8,128)} %param.10, f32[8,512,1024]{2,1,0:T(8,128)} %param.9, f32[]{:T(128)S(6)} %sub.93, f32[]{:T(128)} %bitcast.33, f32[]{:T(128)S(6)} %sub.91, f32[]{:T(128)} %bitcast.27, f32[]{:T(128)S(6)} %sub.90, ...), kind=kLoop, calls=%fused_computation.32 | loop fusion | flops 10481664 | bytes 16793632 | tf_op jit(solution)/shard_map/reduce_max | solution.py:52
  72.2 4.4 fusion.12
  81.9 4.3 fusion.11
  86.3 16.5 %collective-permute-done.10 = bf16[512,1024]{1,0:T(8,128)(2,1)} collective-permute-done((bf16[512,1024]{1,0:T(8,128)(2,1)S(1)}, bf16[512,1024]{1,0:T(8,128)(2,1)}, u32[]{:S(2)}, u32[]{:S(2)}) %collective-permute-start.10) | collective-permute-done | bytes 1048608 | tf_op jit(solution)/shard_map/ppermute | solution.py:9
  104.0 4.4 fusion.10
  131.5 4.4 fusion.9
  135.9 11.2 %collective-permute-done.14 = bf16[512,1024]{1,0:T(8,128)(2,1)} collective-permute-done((bf16[512,1024]{1,0:T(8,128)(2,1)}, bf16[512,1024]{1,0:T(8,128)(2,1)}, u32[]{:S(2)}, u32[]{:S(2)}) %collective-permute-start.14) | collective-permute-done | bytes 1048608 | tf_op jit(solution)/shard_map/ppermute | solution.py:9
  149.8 4.5 fusion.8
  163.9 9.5 %collective-permute-done.18 = bf16[512,1024]{1,0:T(8,128)(2,1)S(1)} collective-permute-done((bf16[512,1024]{1,0:T(8,128)(2,1)}, bf16[512,1024]{1,0:T(8,128)(2,1)S(1)}, u32[]{:S(2)}, u32[]{:S(2)}) %collective-permute-start.18) | collective-permute-done | bytes 1048608 | tf_op jit(solution)/shard_map/ppermute | solution.py:9
  174.7 3.4 fusion.7
  178.1 16.4 %collective-permute-done.21 = bf16[512,1024]{1,0:T(8,128)(2,1)} collective-permute-done((bf16[512,1024]{1,0:T(8,128)(2,1)S(1)}, bf16[512,1024]{1,0:T(8,128)(2,1)}, u32[]{:S(2)}, u32[]{:S(2)}) %collective-permute-start.21) | collective-permute-done | bytes 1048608 | tf_op jit(solution)/shard_map/ppermute | solution.py:9
  195.8 3.4 fusion.6
  217.2 8.4 %collective-permute-done.22 = bf16[512,1024]{1,0:T(8,128)(2,1)} collective-permute-done((bf16[512,1024]{1,0:T(8,128)(2,1)}, bf16[512,1024]{1,0:T(8,128)(2,1)}, u32[]{:S(2)}, u32[]{:S(2)}) %collective-permute-start.22) | collective-permute-done | bytes 1048608 | tf_op jit(solution)/shard_map/ppermute | solution.py:9
  235.2 12.4 %collective-permute-done.25 = bf16[512,1024]{1,0:T(8,128)(2,1)} collective-permute-done((bf16[512,1024]{1,0:T(8,128)(2,1)}, bf16[512,1024]{1,0:T(8,128)(2,1)}, u32[]{:S(2)}, u32[]{:S(2)}) %collective-permute-start.25) | collective-permute-done | bytes 1048608 | tf_op jit(solution)/shard_map/ppermute | solution.py:9
  251.9 4.4 fusion.5
  262.2 4.4 fusion.4
  268.8 4.9 %collective-permute-done.26 = bf16[512,1024]{1,0:T(8,128)(2,1)} collective-permute-done((bf16[512,1024]{1,0:T(8,128)(2,1)S(1)}, bf16[512,1024]{1,0:T(8,128)(2,1)}, u32[]{:S(2)}, u32[]{:S(2)}) %collective-permute-start.26) | collective-permute-done | bytes 1048608 | tf_op jit(solution)/shard_map/ppermute | solution.py:9
  277.6 3.4 fusion.3
  281.0 13.9 %collective-permute-done.29 = bf16[512,1024]{1,0:T(8,128)(2,1)} collective-permute-done((bf16[512,1024]{1,0:T(8,128)(2,1)S(1)}, bf16[512,1024]{1,0:T(8,128)(2,1)}, u32[]{:S(2)}, u32[]{:S(2)}) %collective-permute-start.29) | collective-permute-done | bytes 1048608 | tf_op jit(solution)/shard_map/ppermute | solution.py:9
  302.2 3.4 fusion.2
  325.5 3.4 fusion.1
  328.9 18.5 %collective-permute-done.49 = bf16[512,1024]{1,0:T(8,128)(2,1)} collective-permute-done((bf16[512,1024]{1,0:T(8,128)(2,1)}, bf16[512,1024]{1,0:T(8,128)(2,1)}, u32[]{:S(2)}, u32[]{:S(2)}) %collective-permute-start.49) | collective-permute-done | bytes 1048608 | tf_op jit(solution)/shard_map/ppermute | solution.py:9
  348.6 3.4 fusion
  372.4 5.7 %collective-permute-done.33 = bf16[512,1024]{1,0:T(8,128)(2,1)S(1)} collective-permute-done((bf16[512,1024]{1,0:T(8,128)(2,1)S(1)}, bf16[512,1024]{1,0:T(8,128)(2,1)S(1)}, u32[]{:S(2)}, u32[]{:S(2)}) %collective-permute-start.33) | collective-permute-done | bytes 1048608 | tf_op jit(solution)/shard_map/ppermute | solution.py:9
  378.1 22.0 %collective-permute-done.52 = bf16[512,1024]{1,0:T(8,128)(2,1)S(1)} collective-permute-done((bf16[512,1024]{1,0:T(8,128)(2,1)S(1)}, bf16[512,1024]{1,0:T(8,128)(2,1)S(1)}, u32[]{:S(2)}, u32[]{:S(2)}) %collective-permute-start.52) | collective-permute-done | bytes 1048608 | tf_op jit(solution)/shard_map/ppermute | solution.py:9
  412.4 13.7 %collective-permute-done.36 = bf16[512,1024]{1,0:T(8,128)(2,1)S(1)} collective-permute-done((bf16[512,1024]{1,0:T(8,128)(2,1)S(1)}, bf16[512,1024]{1,0:T(8,128)(2,1)S(1)}, u32[]{:S(2)}, u32[]{:S(2)}) %collective-permute-start.36) | collective-permute-done | bytes 1048608 | tf_op jit(solution)/shard_map/ppermute | solution.py:9
  426.1 22.0 %collective-permute-done.55 = bf16[512,1024]{1,0:T(8,128)(2,1)S(1)} collective-permute-done((bf16[512,1024]{1,0:T(8,128)(2,1)S(1)}, bf16[512,1024]{1,0:T(8,128)(2,1)S(1)}, u32[]{:S(2)}, u32[]{:S(2)}) %collective-permute-start.55) | collective-permute-done | bytes 1048608 | tf_op jit(solution)/shard_map/ppermute | solution.py:9
  (233 shorter events, 176.1 us)
Async XLA Ops:
  32.4 76.0 %collective-permute-start.3 = (bf16[512,1024]{1,0:T(8,128)(2,1)S(1)}, bf16[512,1024]{1,0:T(8,128)(2,1)}, u32[]{:S(2)}, u32[]{:S(2)}) collective-permute-start(bf16[512,1024]{1,0:T(8,128)(2,1)S(1)} %fusion.15), channel_id=1, source_target_pairs={{0,1},{1,0},{2,3},{3,2},{4,5},{5,4},{6,7},{7,6},{8,9},{9,8},{10,11... | collective-permute-start | bytes 3145736 | tf_op jit(solution)/shard_map/ppermute | solution.py:9
  37.3 42.2 %collective-permute-start.7 = (bf16[512,1024]{1,0:T(8,128)(2,1)S(1)}, bf16[512,1024]{1,0:T(8,128)(2,1)}, u32[]{:S(2)}, u32[]{:S(2)}) collective-permute-start(bf16[512,1024]{1,0:T(8,128)(2,1)S(1)} %fusion.15), channel_id=1, source_target_pairs={{0,2},{1,3},{2,0},{3,1},{4,6},{5,7},{6,4},{7,5},{8,10},{9,11},{10,... | collective-permute-start | bytes 3145736 | tf_op jit(solution)/shard_map/ppermute | solution.py:9
  77.9 36.3 %collective-permute-start.38 = (bf16[512,1024]{1,0:T(8,128)(2,1)S(1)}, bf16[512,1024]{1,0:T(8,128)(2,1)}, u32[]{:S(2)}, u32[]{:S(2)}) collective-permute-start(bf16[512,1024]{1,0:T(8,128)(2,1)S(1)} %fusion.14), channel_id=1, source_target_pairs={{0,1},{1,0},{2,3},{3,2},{4,5},{5,4},{6,7},{7,6},{8,9},{9,8},{10,11... | collective-permute-start | bytes 3145736 | tf_op jit(solution)/shard_map/ppermute | solution.py:9
  79.6 45.7 %collective-permute-start.9 = (bf16[512,1024]{1,0:T(8,128)(2,1)S(1)}, bf16[512,1024]{1,0:T(8,128)(2,1)}, u32[]{:S(2)}, u32[]{:S(2)}) collective-permute-start(bf16[512,1024]{1,0:T(8,128)(2,1)S(1)} %fusion.13), channel_id=1, source_target_pairs={{0,1},{1,0},{2,3},{3,2},{4,5},{5,4},{6,7},{7,6},{8,9},{9,8},{10,11... | collective-permute-start | bytes 3145736 | tf_op jit(solution)/shard_map/ppermute | solution.py:9
  79.9 45.3 %collective-permute-start.11 = (bf16[512,1024]{1,0:T(8,128)(2,1)S(1)}, bf16[512,1024]{1,0:T(8,128)(2,1)}, u32[]{:S(2)}, u32[]{:S(2)}) collective-permute-start(bf16[512,1024]{1,0:T(8,128)(2,1)S(1)} %fusion.13), channel_id=1, source_target_pairs={{0,2},{1,3},{2,0},{3,1},{4,6},{5,7},{6,4},{7,5},{8,10},{9,11},{10,... | collective-permute-start | bytes 3145736 | tf_op jit(solution)/shard_map/ppermute | solution.py:9
  108.4 38.7 %collective-permute-start.14 = (bf16[512,1024]{1,0:T(8,128)(2,1)}, bf16[512,1024]{1,0:T(8,128)(2,1)}, u32[]{:S(2)}, u32[]{:S(2)}) collective-permute-start(bf16[512,1024]{1,0:T(8,128)(2,1)} %fusion.12), channel_id=1, source_target_pairs={{0,2},{1,3},{2,0},{3,1},{4,6},{5,7},{6,4},{7,5},{8,10},{9,11},{10,... | collective-permute-start | bytes 3145736 | tf_op jit(solution)/shard_map/ppermute | solution.py:9
  114.2 40.0 %collective-permute-start.39 = (bf16[512,1024]{1,0:T(8,128)(2,1)}, bf16[512,1024]{1,0:T(8,128)(2,1)}, u32[]{:S(2)}, u32[]{:S(2)}) collective-permute-start(bf16[512,1024]{1,0:T(8,128)(2,1)} %collective-permute-done.10), channel_id=1, source_target_pairs={{0,1},{1,0},{2,3},{3,2},{4,5},{5,4},{6,7},{7,6},{8,9},{9,8},{10,11... | collective-permute-start | bytes 3145736 | tf_op jit(solution)/shard_map/ppermute | solution.py:9
  119.0 40.4 %collective-permute-start.40 = (bf16[512,1024]{1,0:T(8,128)(2,1)}, bf16[512,1024]{1,0:T(8,128)(2,1)}, u32[]{:S(2)}, u32[]{:S(2)}) collective-permute-start(bf16[512,1024]{1,0:T(8,128)(2,1)} %fusion.12), channel_id=1, source_target_pairs={{0,1},{1,0},{2,3},{3,2},{4,5},{5,4},{6,7},{7,6},{8,9},{9,8},{10,11... | collective-permute-start | bytes 3145736 | tf_op jit(solution)/shard_map/ppermute | solution.py:9
  125.2 73.9 %collective-permute-start.12 = (bf16[512,1024]{1,0:T(8,128)(2,1)}, bf16[512,1024]{1,0:T(8,128)(2,1)}, u32[]{:S(2)}, u32[]{:S(2)}) collective-permute-start(bf16[512,1024]{1,0:T(8,128)(2,1)} %collective-permute-done.11), channel_id=1, source_target_pairs={{0,1},{1,0},{2,3},{3,2},{4,5},{5,4},{6,7},{7,6},{8,9},{9,8},{10,11... | collective-permute-start | bytes 3145736 | tf_op jit(solution)/shard_map/ppermute | solution.py:9
  129.8 75.5 %collective-permute-start.13 = (bf16[512,1024]{1,0:T(8,128)(2,1)}, bf16[512,1024]{1,0:T(8,128)(2,1)}, u32[]{:S(2)}, u32[]{:S(2)}) collective-permute-start(bf16[512,1024]{1,0:T(8,128)(2,1)} %fusion.11), channel_id=1, source_target_pairs={{0,1},{1,0},{2,3},{3,2},{4,5},{5,4},{6,7},{7,6},{8,9},{9,8},{10,11... | collective-permute-start | bytes 3145736 | tf_op jit(solution)/shard_map/ppermute | solution.py:9
  154.2 40.3 %collective-permute-start.21 = (bf16[512,1024]{1,0:T(8,128)(2,1)S(1)}, bf16[512,1024]{1,0:T(8,128)(2,1)}, u32[]{:S(2)}, u32[]{:S(2)}) collective-permute-start(bf16[512,1024]{1,0:T(8,128)(2,1)S(1)} %copy-done), channel_id=1, source_target_pairs={{0,2},{1,3},{2,0},{3,1},{4,6},{5,7},{6,4},{7,5},{8,10},{9,11},{10,... | collective-permute-start | bytes 3145736 | tf_op jit(solution)/shard_map/ppermute | solution.py:9
  159.4 49.4 %collective-permute-start.41 = (bf16[512,1024]{1,0:T(8,128)(2,1)}, bf16[512,1024]{1,0:T(8,128)(2,1)}, u32[]{:S(2)}, u32[]{:S(2)}) collective-permute-start(bf16[512,1024]{1,0:T(8,128)(2,1)} %collective-permute-done.14), channel_id=1, source_target_pairs={{0,1},{1,0},{2,3},{3,2},{4,5},{5,4},{6,7},{7,6},{8,9},{9,8},{10,11... | collective-permute-start | bytes 3145736 | tf_op jit(solution)/shard_map/ppermute | solution.py:9
  173.4 39.2 %collective-permute-start.42 = (bf16[512,1024]{1,0:T(8,128)(2,1)S(1)}, bf16[512,1024]{1,0:T(8,128)(2,1)}, u32[]{:S(2)}, u32[]{:S(2)}) collective-permute-start(bf16[512,1024]{1,0:T(8,128)(2,1)S(1)} %copy-done), channel_id=1, source_target_pairs={{0,1},{1,0},{2,3},{3,2},{4,5},{5,4},{6,7},{7,6},{8,9},{9,8},{10,11... | collective-permute-start | bytes 3145736 | tf_op jit(solution)/shard_map/ppermute | solution.py:9
  208.8 38.8 %collective-permute-start.25 = (bf16[512,1024]{1,0:T(8,128)(2,1)}, bf16[512,1024]{1,0:T(8,128)(2,1)}, u32[]{:S(2)}, u32[]{:S(2)}) collective-permute-start(bf16[512,1024]{1,0:T(8,128)(2,1)} %fusion.8), channel_id=1, source_target_pairs={{0,2},{1,3},{2,0},{3,1},{4,6},{5,7},{6,4},{7,5},{8,10},{9,11},{10,... | collective-permute-start | bytes 3145736 | tf_op jit(solution)/shard_map/ppermute | solution.py:9
  212.6 36.5 %collective-permute-start.43 = (bf16[512,1024]{1,0:T(8,128)(2,1)}, bf16[512,1024]{1,0:T(8,128)(2,1)}, u32[]{:S(2)}, u32[]{:S(2)}) collective-permute-start(bf16[512,1024]{1,0:T(8,128)(2,1)} %collective-permute-done.21), channel_id=1, source_target_pairs={{0,1},{1,0},{2,3},{3,2},{4,5},{5,4},{6,7},{7,6},{8,9},{9,8},{10,11... | collective-permute-start | bytes 3145736 | tf_op jit(solution)/shard_map/ppermute | solution.py:9
  225.6 49.4 %collective-permute-start.23 = (bf16[512,1024]{1,0:T(8,128)(2,1)}, bf16[512,1024]{1,0:T(8,128)(2,1)S(1)}, u32[]{:S(2)}, u32[]{:S(2)}) collective-permute-start(bf16[512,1024]{1,0:T(8,128)(2,1)} %collective-permute-done.22), channel_id=1, source_target_pairs={{0,1},{1,0},{2,3},{3,2},{4,5},{5,4},{6,7},{7,6},{8,9},{9,8},{10,11... | collective-permute-start | bytes 3145736 | tf_op jit(solution)/shard_map/ppermute | solution.py:9
  233.9 62.2 %collective-permute-start.24 = (bf16[512,1024]{1,0:T(8,128)(2,1)S(1)}, bf16[512,1024]{1,0:T(8,128)(2,1)}, u32[]{:S(2)}, u32[]{:S(2)}) collective-permute-start(bf16[512,1024]{1,0:T(8,128)(2,1)S(1)} %fusion.7), channel_id=1, source_target_pairs={{0,1},{1,0},{2,3},{3,2},{4,5},{5,4},{6,7},{7,6},{8,9},{9,8},{10,11... | collective-permute-start | bytes 3145736 | tf_op jit(solution)/shard_map/ppermute | solution.py:9
  249.1 45.8 %collective-permute-start.29 = (bf16[512,1024]{1,0:T(8,128)(2,1)S(1)}, bf16[512,1024]{1,0:T(8,128)(2,1)}, u32[]{:S(2)}, u32[]{:S(2)}) collective-permute-start(bf16[512,1024]{1,0:T(8,128)(2,1)S(1)} %fusion.6), channel_id=1, source_target_pairs={{0,2},{1,3},{2,0},{3,1},{4,6},{5,7},{6,4},{7,5},{8,10},{9,11},{10,... | collective-permute-start | bytes 3145736 | tf_op jit(solution)/shard_map/ppermute | solution.py:9
  259.8 45.8 %collective-permute-start.45 = (bf16[512,1024]{1,0:T(8,128)(2,1)}, bf16[512,1024]{1,0:T(8,128)(2,1)}, u32[]{:S(2)}, u32[]{:S(2)}) collective-permute-start(bf16[512,1024]{1,0:T(8,128)(2,1)} %collective-permute-done.25), channel_id=1, source_target_pairs={{0,1},{1,0},{2,3},{3,2},{4,5},{5,4},{6,7},{7,6},{8,9},{9,8},{10,11... | collective-permute-start | bytes 3145736 | tf_op jit(solution)/shard_map/ppermute | solution.py:9
  273.7 39.4 %collective-permute-start.46 = (bf16[512,1024]{1,0:T(8,128)(2,1)S(1)}, bf16[512,1024]{1,0:T(8,128)(2,1)}, u32[]{:S(2)}, u32[]{:S(2)}) collective-permute-start(bf16[512,1024]{1,0:T(8,128)(2,1)S(1)} %fusion.6), channel_id=1, source_target_pairs={{0,1},{1,0},{2,3},{3,2},{4,5},{5,4},{6,7},{7,6},{8,9},{9,8},{10,11... | collective-permute-start | bytes 3145736 | tf_op jit(solution)/shard_map/ppermute | solution.py:9
  275.0 77.0 %collective-permute-start.27 = (bf16[512,1024]{1,0:T(8,128)(2,1)}, bf16[512,1024]{1,0:T(8,128)(2,1)}, u32[]{:S(2)}, u32[]{:S(2)}) collective-permute-start(bf16[512,1024]{1,0:T(8,128)(2,1)} %collective-permute-done.26), channel_id=1, source_target_pairs={{0,1},{1,0},{2,3},{3,2},{4,5},{5,4},{6,7},{7,6},{8,9},{9,8},{10,11... | collective-permute-start | bytes 3145736 | tf_op jit(solution)/shard_map/ppermute | solution.py:9
  294.9 62.2 %collective-permute-start.28 = (bf16[512,1024]{1,0:T(8,128)(2,1)}, bf16[512,1024]{1,0:T(8,128)(2,1)}, u32[]{:S(2)}, u32[]{:S(2)}) collective-permute-start(bf16[512,1024]{1,0:T(8,128)(2,1)} %fusion.5), channel_id=1, source_target_pairs={{0,1},{1,0},{2,3},{3,2},{4,5},{5,4},{6,7},{7,6},{8,9},{9,8},{10,11... | collective-permute-start | bytes 3145736 | tf_op jit(solution)/shard_map/ppermute | solution.py:9
  313.1 48.8 %collective-permute-start.47 = (bf16[512,1024]{1,0:T(8,128)(2,1)}, bf16[512,1024]{1,0:T(8,128)(2,1)}, u32[]{:S(2)}, u32[]{:S(2)}) collective-permute-start(bf16[512,1024]{1,0:T(8,128)(2,1)} %collective-permute-done.29), channel_id=1, source_target_pairs={{0,1},{1,0},{2,3},{3,2},{4,5},{5,4},{6,7},{7,6},{8,9},{9,8},{10,11... | collective-permute-start | bytes 3145736 | tf_op jit(solution)/shard_map/ppermute | solution.py:9
  324.3 43.6 %collective-permute-start.48 = (bf16[512,1024]{1,0:T(8,128)(2,1)}, bf16[512,1024]{1,0:T(8,128)(2,1)}, u32[]{:S(2)}, u32[]{:S(2)}) collective-permute-start(bf16[512,1024]{1,0:T(8,128)(2,1)} %fusion.4), channel_id=1, source_target_pairs={{0,1},{1,0},{2,3},{3,2},{4,5},{5,4},{6,7},{7,6},{8,9},{9,8},{10,11... | collective-permute-start | bytes 3145736 | tf_op jit(solution)/shard_map/ppermute | solution.py:9
  347.4 55.4 %collective-permute-start.32 = (bf16[512,1024]{1,0:T(8,128)(2,1)S(1)}, bf16[512,1024]{1,0:T(8,128)(2,1)}, u32[]{:S(2)}, u32[]{:S(2)}) collective-permute-start(bf16[512,1024]{1,0:T(8,128)(2,1)S(1)} %fusion.3), channel_id=1, source_target_pairs={{0,1},{1,0},{2,3},{3,2},{4,5},{5,4},{6,7},{7,6},{8,9},{9,8},{10,11... | collective-permute-start | bytes 3145736 | tf_op jit(solution)/shard_map/ppermute | solution.py:9
  357.1 43.0 %collective-permute-start.31 = (bf16[512,1024]{1,0:T(8,128)(2,1)}, bf16[512,1024]{1,0:T(8,128)(2,1)S(1)}, u32[]{:S(2)}, u32[]{:S(2)}) collective-permute-start(bf16[512,1024]{1,0:T(8,128)(2,1)} %collective-permute-done.30), channel_id=1, source_target_pairs={{0,1},{1,0},{2,3},{3,2},{4,5},{5,4},{6,7},{7,6},{8,9},{9,8},{10,11... | collective-permute-start | bytes 3145736 | tf_op jit(solution)/shard_map/ppermute | solution.py:9
  361.9 38.2 %collective-permute-start.52 = (bf16[512,1024]{1,0:T(8,128)(2,1)S(1)}, bf16[512,1024]{1,0:T(8,128)(2,1)S(1)}, u32[]{:S(2)}, u32[]{:S(2)}) collective-permute-start(bf16[512,1024]{1,0:T(8,128)(2,1)S(1)} %fusion.2), channel_id=1, source_target_pairs={{0,2},{1,3},{2,0},{3,1},{4,6},{5,7},{6,4},{7,5},{8,10},{9,11},{10,... | collective-permute-start | bytes 3145736 | tf_op jit(solution)/shard_map/ppermute | solution.py:9
  367.9 38.3 %collective-permute-start.50 = (bf16[512,1024]{1,0:T(8,128)(2,1)}, bf16[512,1024]{1,0:T(8,128)(2,1)S(1)}, u32[]{:S(2)}, u32[]{:S(2)}) collective-permute-start(bf16[512,1024]{1,0:T(8,128)(2,1)} %collective-permute-done.49), channel_id=1, source_target_pairs={{0,1},{1,0},{2,3},{3,2},{4,5},{5,4},{6,7},{7,6},{8,9},{9,8},{10,11... | collective-permute-start | bytes 3145736 | tf_op jit(solution)/shard_map/ppermute | solution.py:9
  400.1 52.2 %collective-permute-start.35 = (bf16[512,1024]{1,0:T(8,128)(2,1)S(1)}, bf16[512,1024]{1,0:T(8,128)(2,1)S(1)}, u32[]{:S(2)}, u32[]{:S(2)}) collective-permute-start(bf16[512,1024]{1,0:T(8,128)(2,1)S(1)} %fusion.1), channel_id=1, source_target_pairs={{0,1},{1,0},{2,3},{3,2},{4,5},{5,4},{6,7},{7,6},{8,9},{9,8},{10,11... | collective-permute-start | bytes 3145736 | tf_op jit(solution)/shard_map/ppermute | solution.py:9
  406.3 41.9 %collective-permute-start.55 = (bf16[512,1024]{1,0:T(8,128)(2,1)S(1)}, bf16[512,1024]{1,0:T(8,128)(2,1)S(1)}, u32[]{:S(2)}, u32[]{:S(2)}) collective-permute-start(bf16[512,1024]{1,0:T(8,128)(2,1)S(1)} %fusion), channel_id=1, source_target_pairs={{0,2},{1,3},{2,0},{3,1},{4,6},{5,7},{6,4},{7,5},{8,10},{9,11},{10,... | collective-permute-start | bytes 3145736 | tf_op jit(solution)/shard_map/ppermute | solution.py:9
  409.8 40.4 %collective-permute-start.53 = (bf16[512,1024]{1,0:T(8,128)(2,1)S(1)}, bf16[512,1024]{1,0:T(8,128)(2,1)S(1)}, u32[]{:S(2)}, u32[]{:S(2)}) collective-permute-start(bf16[512,1024]{1,0:T(8,128)(2,1)S(1)} %collective-permute-done.52), channel_id=1, source_target_pairs={{0,1},{1,0},{2,3},{3,2},{4,5},{5,4},{6,7},{7,6},{8,9},{9,8},{10,11... | collective-permute-start | bytes 3145736 | tf_op jit(solution)/shard_map/ppermute | solution.py:9
  411.9 42.5 %collective-permute-start.54 = (bf16[512,1024]{1,0:T(8,128)(2,1)S(1)}, bf16[512,1024]{1,0:T(8,128)(2,1)S(1)}, u32[]{:S(2)}, u32[]{:S(2)}) collective-permute-start(bf16[512,1024]{1,0:T(8,128)(2,1)S(1)} %fusion), channel_id=1, source_target_pairs={{0,1},{1,0},{2,3},{3,2},{4,5},{5,4},{6,7},{7,6},{8,9},{9,8},{10,11... | collective-permute-start | bytes 3145736 | tf_op jit(solution)/shard_map/ppermute | solution.py:9
  (36 other events, 532.9 us)
